TPU v7x, 32 devices: a whole 2x2x4 slice. The times are simulated.
32 devices in a mesh: trial: 4 (over y, x), rows: 2 (over core), cols: 4 (over z).
Axes of the slice: x: 2, y: 2, z: 4, core: 2. Of those that a mesh axis runs over, the one named last changes fastest.
Arguments:
- weight_gate: float32 [8192, 8192], P(('trial', 'rows'), 'cols'), parts along dimension 0, may hold values from -0.1875 to 0.1875
- moment_gate: float32 [8192, 8192], P(('trial', 'rows'), 'cols'), parts along dimension 0, may hold values from -6 to 6
- square_gate: float32 [8192, 8192], P(('trial', 'rows'), 'cols'), parts along dimension 0, may hold values from 0.1 to 10
- weight_up: float32 [8192, 8192], P(('trial', 'rows'), 'cols'), parts along dimension 0, may hold values from -0.1875 to 0.1875
- moment_up: float32 [8192, 8192], P(('trial', 'rows'), 'cols'), parts along dimension 0, may hold values from -6 to 6
- square_up: float32 [8192, 8192], P(('trial', 'rows'), 'cols'), parts along dimension 0, may hold values from 0.1 to 10
- norm_gain: float32 [8192], P(('trial', 'rows')), parts along dimension 0, may hold values from 0.25 to 1.75
Outputs:
- serving_gate: bfloat16 [8192, 8192], P('trial', 'cols'), parts along dimension 0
- serving_up: bfloat16 [8192, 8192], P('trial', 'cols'), parts along dimension 0
- column_gate: float32 [32768], P(('trial', 'cols')), parts along dimension 0
- column_up: float32 [32768], P(('trial', 'cols')), parts along dimension 0
There are 4 independent parts, one for each index of `trial`. A program takes and returns all parts, laid end to end along the dimension named above; each array names one. Nothing has to cross between parts.
All inputs are finite; a program needn't handle non-finite values. Where the computation divides by a largest or mean magnitude, that divisor is 1e-20 or more.
Results may differ from a plain program's by a relative error of at most 0.001.
Values may be sent and summed in bfloat16 or wider, within the bound.
No kernel may reach another device: no remote copies, remote signals or barrier semaphores. Data moves between devices by JAX's collectives and lax.ppermute only.
A program may use at most 128 MiB of HBM per device.

v0:
```python
import jax
import jax.numpy as jnp
from jax import lax
from jax.sharding import PartitionSpec as P

D_MODEL = 2048


learn_rate = 0.02
decay_rate = 0.05
tiny_value = 1e-08


def shards(weight_gate, moment_gate, square_gate, weight_up, moment_up, square_up, norm_gain):
    whole_gate = weight_gate - learn_rate * (
        moment_gate / (jnp.sqrt(square_gate) + tiny_value) + decay_rate * weight_gate
    )
    whole_up = weight_up - learn_rate * (
        moment_up / (jnp.sqrt(square_up) + tiny_value) + decay_rate * weight_up
    )
    whole_gained_gate = whole_gate * norm_gain[:, None]
    whole_gained_up = whole_up * norm_gain[:, None]
    total_gate, total_up = lax.psum(
        (jnp.sum(jnp.abs(whole_gained_gate), axis=0), jnp.sum(jnp.abs(whole_gained_up), axis=0)),
        "rows",
    )
    column_gate = total_gate / D_MODEL
    column_up = total_up / D_MODEL
    narrow_gate, narrow_up = (
        (whole_gained_gate / column_gate).astype(jnp.bfloat16),
        (whole_gained_up / column_up).astype(jnp.bfloat16),
    )
    serving_gate, serving_up = (
        lax.all_gather(narrow_gate, "rows", axis=0, tiled=True),
        lax.all_gather(narrow_up, "rows", axis=0, tiled=True),
    )
    return (serving_gate, serving_up, column_gate, column_up)


def solution(mesh):
    return jax.shard_map(
        shards,
        mesh=mesh,
        in_specs=(
            P(("trial", "rows"), "cols"),
            P(("trial", "rows"), "cols"),
            P(("trial", "rows"), "cols"),
            P(("trial", "rows"), "cols"),
            P(("trial", "rows"), "cols"),
            P(("trial", "rows"), "cols"),
            P(("trial", "rows")),
        ),
        out_specs=(
            P("trial", "cols"),
            P("trial", "cols"),
            P(("trial", "cols")),
            P(("trial", "cols")),
        ),
        check_vma=False,
    )
```

profile of v0, /device:TPU:3, one launch (start us, length us, event | category | flops | bytes accessed | tf_op | source)
XLA Modules:
  0.0 111.3 jit_solution(3213533298670833020)
XLA Ops:
  7.2 0.0 all-gather.3.cloned.1.call-start
  7.2 25.5 %abs_reduce_fusion = (f32[2048]{0:T(1024)S(1)}, f32[1024,2048]{1,0:T(8,128)}, f32[2048]{0:T(1024)S(1)}, f32[1024,2048]{1,0:T(8,128)}) fusion(f32[1024]{0:T(1024)} %param.13, f32[1024,2048]{1,0:T(8,128)} %param.10, f32[1024,2048]{1,0:T(8,128)} %param.11, f32[1024,2048]{1,0:T(8,128)} %param.12, f32[1024,2048]{1,0:T(8,128)} %param.7, f32[1024,2048]{1,0:T(8,128)} %param.8, ...), kind=kLoop, calls=%fused_computation.1 | loop fusion | flops 37744640 | bytes 67129344 | tf_op jit(solution)/shard_map/reduce_sum | solution.py:24
  32.7 3.8 %all-reduce = (f32[2048]{0:T(1024)S(1)}, f32[2048]{0:T(1024)S(1)}) all-reduce(f32[2048]{0:T(1024)S(1)} %get-tuple-element.10, f32[2048]{0:T(1024)S(1)} %get-tuple-element.6), channel_id=1, replica_groups=mesh['trial'=4,'rows'=2,'cols'=4] {'rows'}, use_global_device_ids=true, to_apply=%region_1.0 | all-reduce | flops 4096 | bytes 32768 | tf_op jit(solution)/shard_map/psum | solution.py:23
  36.5 0.0 copy-start
  36.5 6.5 %divide_convert_fusion.1 = bf16[1024,2048]{1,0:T(8,128)(2,1)} fusion(f32[1024,2048]{1,0:T(8,128)} %get-tuple-element.11, f32[2048]{0:T(1024)S(1)} %broadcast_multiply_fusion.1), kind=kLoop, calls=%fused_computation.3 | loop fusion | flops 4194304 | bytes 12591104 | tf_op jit(solution)/shard_map/convert_element_type | solution.py:30
  43.0 0.0 all-gather.3.cloned.1.call-update
  43.0 0.0 copy-done
  43.0 0.0 all-gather.5.cloned.1.call-start
  43.1 0.0 copy-start.1
  43.1 6.6 %divide_convert_fusion = bf16[1024,2048]{1,0:T(8,128)(2,1)} fusion(f32[1024,2048]{1,0:T(8,128)} %get-tuple-element.7, f32[2048]{0:T(1024)S(1)} %broadcast_multiply_fusion), kind=kLoop, calls=%fused_computation | loop fusion | flops 4194304 | bytes 12591104 | tf_op jit(solution)/shard_map/convert_element_type | solution.py:31
  49.7 0.0 all-gather.5.cloned.1.call-update
  49.7 0.0 copy-done.1
  49.7 14.8 %all-gather.3.cloned.1.call-done = bf16[2048,2048]{1,0:T(8,128)(2,1)} async-done(((bf16[1024,2048]{1,0:T(8,128)(2,1)}), bf16[2048,2048]{1,0:T(8,128)(2,1)}) %all-gather.3.cloned.1.call-update) | async-done | bytes 8388624 | tf_op jit(solution)/shard_map/all_gather | solution.py:34
  64.4 23.2 %all-gather.5.cloned.1.call-done = bf16[2048,2048]{1,0:T(8,128)(2,1)} async-done(((bf16[1024,2048]{1,0:T(8,128)(2,1)}), bf16[2048,2048]{1,0:T(8,128)(2,1)}) %all-gather.5.cloned.1.call-update) | async-done | bytes 8388624 | tf_op jit(solution)/shard_map/all_gather | solution.py:35
  87.6 8.4 %copy.13 = bf16[2048,2048]{1,0:T(8,128)(2,1)} copy(bf16[2048,2048]{1,0:T(8,128)(2,1)} %all-gather.3.cloned.1.call-done) | data formatting | bytes 16777216
  96.1 8.4 %copy.14 = bf16[2048,2048]{1,0:T(8,128)(2,1)} copy(bf16[2048,2048]{1,0:T(8,128)(2,1)} %all-gather.5.cloned.1.call-done) | data formatting | bytes 16777216
  (2 shorter events, 0.0 us)
Async XLA Ops:
  7.2 57.3 %all-gather.3.cloned.1.call-start = ((), (), s32[]{:S(2)}) async-start(), calls=%async_computation | async-start | bytes 12582912 | tf_op jit(solution)/shard_map/all_gather | solution.py:34
  36.5 6.5 %copy-start = (f32[2048]{0:T(1024)}, f32[2048]{0:T(1024)S(1)}, u32[]{:S(2)}) copy-start(f32[2048]{0:T(1024)S(1)} %broadcast_multiply_fusion.1) | copy-start | bytes 24580
  43.0 44.6 %all-gather.5.cloned.1.call-start = ((), (), s32[]{:S(2)}) async-start(), calls=%async_computation.1 | async-start | bytes 12582912 | tf_op jit(solution)/shard_map/all_gather | solution.py:35
  43.1 6.6 %copy-start.1 = (f32[2048]{0:T(1024)}, f32[2048]{0:T(1024)S(1)}, u32[]{:S(2)}) copy-start(f32[2048]{0:T(1024)S(1)} %broadcast_multiply_fusion) | copy-start | bytes 24580
Sparse Core Ops, SparseCore 0:
  43.1 21.2 all-gather.2
  66.6 21.0 all-gather.4
where the time goes:
time: 112 us; the launch traced here: 111 us
  other arithmetic  38.5 us (34%)
  waiting for transfers between devices  38 us (34%)
  local copies, waits for them, and re-layouts  16.9 us (15%)
  between operations  14.1 us (13%)
  blocking collectives  3.79 us (3%)
    reduce_sum x1, other arithmetic, shards(): jnp.sum(jnp.abs(whole_gained_up), axis=0)  25.5 us
    all_gather x1, waiting for transfers between devices, shards(): lax.all_gather(narrow_up, 'rows', axis=0, tiled=True)  23.2 us
    unnamed x6, local copies, waits for them, and re-layouts  16.9 us
    all_gather x1, waiting for transfers between devices, shards(): lax.all_gather(narrow_gate, 'rows', axis=0, tiled=True)  14.8 us
    convert_element_type x1, other arithmetic, shards(): (whole_gained_up / column_up).astype(jnp.bfloat16)  6.57 us
    convert_element_type x1, other arithmetic, shards(): (whole_gained_gate / column_gate).astype(jnp.bfloat16)  6.49 us
    psum x1, blocking collectives, shards(): lax.psum((jnp.sum(jnp.abs(whole_gained_gate), axis=0), jnp.sum(jnp.abs(wh...  3.79 us
  transfers between devices with their start and end apart: 2, of which 2 were waited for; matrix products, arithmetic and copies ran while one was open for 6% of the time, Pallas kernels for 0%

commit v1 on v0

v1 whole, which is shorter than its diff:
```python
import functools

import jax
import jax.numpy as jnp
from jax import lax
from jax.experimental import pallas as pl
from jax.experimental.pallas import tpu as pltpu
from jax.sharding import PartitionSpec as P

learn_rate = 0.02
decay_rate = 0.05
tiny_value = 1e-08
keep_rate = 1.0 - learn_rate * decay_rate

UNITS = 2
FOLD = 2
LANES = 128


def update_kernel(
    after_ref, gain_ref, weight_ref, moment_ref, square_ref, gained_ref, sums_ref, part_ref, spread_ref, *, block, fold
):
    step = pl.program_id(0)
    width = weight_ref.shape[1]

    def spread(at, slot):
        for n in range(fold):
            line = gain_ref[pl.ds(at * fold + n, 1), :]
            spread_ref[slot, n * block : (n + 1) * block, :] = jnp.broadcast_to(line, (LANES, block)).T

    @pl.when(step == 0)
    def _():
        part_ref[...] = jnp.zeros_like(part_ref)
        spread(0, 0)

    spread(jnp.minimum(step + 1, pl.num_programs(0) - 1), (step + 1) % 2)
    for n in range(fold):
        inner = slice(n * block, (n + 1) * block)
        rows = pl.ds(pl.multiple_of((step * fold + n) * block, block), block)
        gain = spread_ref[step % 2, inner, :]
        keep = keep_rate * gain
        move = learn_rate * gain
        for at in range(0, width, LANES):
            lanes = slice(at, at + LANES)
            square = square_ref[inner, lanes]
            divisor = square * lax.rsqrt(square) + tiny_value
            direction = moment_ref[inner, lanes] * lax.rsqrt(divisor * divisor)
            gained = keep * weight_ref[inner, lanes] - move * direction
            gained_ref[rows, lanes] = gained
            part_ref[:, lanes] += jnp.sum(jnp.abs(gained).reshape(block // 8, 8, LANES), axis=0)

    @pl.when(step == pl.num_programs(0) - 1)
    def _():
        sums_ref[...] = jnp.sum(part_ref[...], axis=0, keepdims=True)


def update(after, gain, weight, moment, square, chunk, width):
    rows = weight.shape[0]
    block = min(rows, LANES)
    fold = FOLD if rows % (block * FOLD) == 0 else 1
    spec = pl.BlockSpec((block * fold, width), lambda i: (i, chunk))
    whole = pl.BlockSpec(memory_space=pltpu.VMEM)
    elements = rows * width
    return pl.pallas_call(
        functools.partial(update_kernel, block=block, fold=fold),
        grid=(rows // block // fold,),
        in_specs=[pl.BlockSpec(memory_space=pl.ANY), whole, spec, spec, spec],
        out_specs=[whole, whole],
        out_shape=[pltpu.VMEM((rows, width), jnp.float32), pltpu.VMEM((1, width), jnp.float32)],
        scratch_shapes=[pltpu.VMEM((8, width), jnp.float32), pltpu.VMEM((2, fold * block, LANES), jnp.float32)],
        compiler_params=pltpu.CompilerParams(vmem_limit_bytes=24 << 20),
        cost_estimate=pl.CostEstimate(flops=elements * 1000, bytes_accessed=elements * 12, transcendentals=elements * 2),
        name="update",
    )(after, *(pltpu.with_memory_space_constraint(array, pltpu.HBM) for array in (gain, weight, moment, square)))


def scale_kernel(*refs, total_rows):
    gained_ref, *sum_refs, narrow_ref, column_ref = refs
    total = sum_refs[0][...]
    for ref in sum_refs[1:]:
        total = total + ref[...]
    column = total / total_rows
    column_ref[...] = column
    inverse = 1.0 / column
    rows, width = gained_ref.shape
    block = min(rows, 64)
    factors = [jnp.broadcast_to(inverse[:, at : at + LANES], (8, LANES)) for at in range(0, width, LANES)]

    def body(i, _):
        here = pl.ds(pl.multiple_of(i * block, block), block)
        for n, factor in enumerate(factors):
            lanes = slice(n * LANES, (n + 1) * LANES)
            values = gained_ref[here, lanes].reshape(block // 8, 8, LANES) * factor
            narrow_ref[here, lanes] = values.reshape(block, LANES).astype(jnp.bfloat16)
        return 0

    lax.fori_loop(0, rows // block, body, 0)


def scale(gained, sums, total_rows):
    rows, width = gained.shape
    whole = pl.BlockSpec(memory_space=pltpu.VMEM)
    elements = rows * width
    return pl.pallas_call(
        functools.partial(scale_kernel, total_rows=total_rows),
        in_specs=[whole] * (1 + len(sums)),
        out_specs=[whole, whole],
        out_shape=[pltpu.VMEM((rows, width), jnp.bfloat16), pltpu.VMEM((1, width), jnp.float32)],
        compiler_params=pltpu.CompilerParams(vmem_limit_bytes=4 << 20),
        cost_estimate=pl.CostEstimate(flops=elements * 200, bytes_accessed=elements, transcendentals=0),
        name="scale",
    )(pltpu.with_memory_space_constraint(gained, pltpu.VMEM), *sums)


def place_kernel(*refs, row_devices, count, n_outs, n_held, where, width):
    parts = refs[:count]
    outs = refs[count + n_held : count + n_held + n_outs]
    me = lax.axis_index("rows")
    sems = refs[-1]
    copies = []
    for n, (out, hop, chunk) in enumerate(where):
        rows = parts[n].shape[0]
        target = outs[out].at[pl.ds(pl.multiple_of(lax.rem(me + (row_devices - hop), row_devices) * rows, rows), rows), pl.ds(chunk * width, width)]
        copies.append(pltpu.make_async_copy(parts[n], target, sems.at[n]))
    for copy in copies:
        copy.start()
    for copy in copies:
        copy.wait()


def place(row_devices, parts, where, held, out_shapes):
    width = parts[0].shape[1]
    n_held = len(held)
    elements = sum(part.size for part in parts)
    return pl.pallas_call(
        functools.partial(
            place_kernel, row_devices=row_devices, count=len(parts), n_outs=len(out_shapes), n_held=n_held, where=tuple(where), width=width
        ),
        in_specs=[pl.BlockSpec(memory_space=pl.ANY)] * (len(parts) + n_held),
        out_specs=[pl.BlockSpec(memory_space=pl.ANY)] * len(out_shapes),
        out_shape=out_shapes,
        input_output_aliases={len(parts) + n: n for n in range(n_held)},
        scratch_shapes=[pltpu.SemaphoreType.DMA((len(parts),))],
        compiler_params=pltpu.CompilerParams(vmem_limit_bytes=1 << 20),
        cost_estimate=pl.CostEstimate(flops=elements * 400, bytes_accessed=elements * 4, transcendentals=0),
        name="place",
    )(*(pltpu.with_memory_space_constraint(part, pltpu.VMEM) for part in parts), *held)


def shards(row_devices, weight_gate, moment_gate, square_gate, weight_up, moment_up, square_up, norm_gain):
    rows, columns = weight_gate.shape
    chunks = UNITS // 2
    width = columns // chunks
    sources = ((weight_gate, moment_gate, square_gate), (weight_up, moment_up, square_up))
    units = [(which, chunk) for which in range(2) for chunk in range(chunks)]
    gain = norm_gain.reshape(-1, min(rows, LANES))

    def rotations(value):
        return [
            lax.ppermute(value, "rows", [(j, (j + hop) % row_devices) for j in range(row_devices)])
            for hop in range(1, row_devices)
        ]

    pieces, scales = [], []
    pending = None
    ready = gain

    def finish(unit, gained, all_sums):
        narrow, column = scale(gained, all_sums, rows * row_devices)
        pieces.append((unit, [narrow] + rotations(narrow)))
        scales.append(column)
        return narrow

    history = []
    for unit in units:
        which, chunk = unit
        if len(history) >= 2:
            ready = finish(*history[len(history) - 2])
        gained, sums = update(ready, gain, *sources[which], chunk, width)
        history.append((unit, gained, [sums] + rotations(sums)))
    for entry in history[max(len(history) - 2, 0):]:
        finish(*entry)

    first, last = [], []
    for n, ((which, chunk), held) in enumerate(pieces):
        for hop, part in enumerate(held):
            group = last if hop > 0 and n == len(pieces) - 1 else first
            group.append((part, (which, hop, chunk)))
    out = jax.ShapeDtypeStruct((rows * row_devices, columns), jnp.bfloat16)
    outs = place(row_devices, [p for p, _ in first], [w for _, w in first], (), [out, out])
    if last:
        outs = [outs[0], *place(row_devices, [p for p, _ in last], [(0, h, c) for _, (_, h, c) in last], (outs[1],), [out])]
    column_gate = jnp.concatenate([c.reshape(-1) for c in scales[:chunks]])
    column_up = jnp.concatenate([c.reshape(-1) for c in scales[chunks:]])
    return (outs[0], outs[1], column_gate, column_up)


def solution(mesh):
    matrix = P(("trial", "rows"), "cols")
    return jax.shard_map(
        functools.partial(shards, mesh.shape["rows"]),
        mesh=mesh,
        in_specs=(matrix,) * 6 + (P(("trial", "rows")),),
        out_specs=(P("trial", "cols"), P("trial", "cols"), P(("trial", "cols")), P(("trial", "cols"))),
        check_vma=False,
    )
```

time: 112 us -> 36.2 us (0.32)
  other arithmetic: 38.5 us -> 0 us
  waiting for transfers between devices: 38 us -> 2.94 us
  Pallas kernels: 0 us -> 29.6 us
  local copies, waits for them, and re-layouts: 16.9 us -> 1.2 us
  between operations: 14.1 us -> 0.68 us
  blocking collectives: 3.79 us -> 0 us
  starting transfers between devices: 0.08 us -> 1.61 us
    all_gather x2 -> x0, waiting for transfers between devices: 37.9 us -> none  [the longest x1 23.2 us: shards(): lax.all_gather(narrow_up, 'rows', axis=0, tiled=True)]
    pallas_call x0 -> x6, Pallas kernels: none -> 29.6 us  [the longest x2 21.4 us: update(): pl.pallas_call(functools.partial(update_kernel, block=block, fold=fold),...]
    reduce_sum x1 -> x0, other arithmetic: 25.5 us -> none  [shards(): jnp.sum(jnp.abs(whole_gained_up), axis=0)]
    unnamed x6 -> x2, local copies, waits for them, and re-layouts: 16.9 us -> 1.2 us
    convert_element_type x2 -> x0, other arithmetic: 13.1 us -> none  [the longest x1 6.57 us: shards(): (whole_gained_up / column_up).astype(jnp.bfloat16)]
    psum x1 -> x0, blocking collectives: 3.79 us -> none  [shards(): lax.psum((jnp.sum(jnp.abs(whole_gained_gate), axis=0), jnp.sum(jnp.abs(wh...]
    ppermute x0 -> x4, waiting for transfers between devices: none -> 2.94 us  [rotations(): lax.ppermute(value, 'rows', [(j, (j + hop) % row_devices) for j in range(...]
    ppermute x0 -> x4, starting transfers between devices: none -> 1.61 us  [rotations(): lax.ppermute(value, 'rows', [(j, (j + hop) % row_devices) for j in range(...]
  transfers between devices with their start and end apart: 2 -> 4, of which waited for: 2 -> 3; matrix products, arithmetic and copies ran while one was open for 6% -> 3% of each run, Pallas kernels for 0% -> 45%
where the time goes in v1:
time: 36.2 us; the launch traced here: 36.1 us
  Pallas kernels  29.6 us (82%)
  waiting for transfers between devices  2.94 us (8%)
  starting transfers between devices  1.61 us (4%)
  local copies, waits for them, and re-layouts  1.2 us (3%)
  between operations  0.68 us (2%)
    pallas_call x2, Pallas kernels, update(): pl.pallas_call(functools.partial(update_kernel, block=block, fold=fold),...  21.4 us
    pallas_call x2, Pallas kernels, place(): pl.pallas_call(functools.partial(place_kernel, row_devices=row_devices, c...  6.7 us
    ppermute x4, waiting for transfers between devices, rotations(): lax.ppermute(value, 'rows', [(j, (j + hop) % row_devices) for j in range(...  2.94 us
    ppermute x4, starting transfers between devices, rotations(): lax.ppermute(value, 'rows', [(j, (j + hop) % row_devices) for j in range(...  1.61 us
    pallas_call x2, Pallas kernels, scale(): pl.pallas_call(functools.partial(scale_kernel, total_rows=total_rows), in...  1.56 us
    unnamed x2, local copies, waits for them, and re-layouts  1.2 us
  transfers between devices with their start and end apart: 4, of which 3 were waited for; matrix products, arithmetic and copies ran while one was open for 3% of the time, Pallas kernels for 45%

profile of v1, /device:TPU:3, one launch (start us, length us, event | category | flops | bytes accessed | tf_op | source)
XLA Modules:
  0.0 36.1 jit_solution(16654179928320913360)
XLA Ops:
  0.6 10.7 %update.2 = (f32[1024,2048]{1,0:T(8,128)S(1)}, f32[1,2048]{1,0:T(1,128)S(1)}) custom-call(f32[8,128]{1,0:T(8,128)} %bitcast.5, f32[8,128]{1,0:T(8,128)} %bitcast.6, f32[1024,2048]{1,0:T(8,128)} %weight_ref.2, f32[1024,2048]{1,0:T(8,128)} %moment_ref.2, f32[1024,2048]{1,0:T(8,128)} %square_ref.2), custom_call_target="tpu_custom_call" | custom-call | flops 2097152000 | bytes 25165824 | tf_op jit(solution)/shard_map/update/pallas_call | solution.py:64
  11.3 0.7 %collective-permute-start = (f32[1,2048]{1,0:T(1,128)S(1)}, f32[1,2048]{1,0:T(1,128)S(1)}, u32[]{:S(2)}, u32[]{:S(2)}) collective-permute-start(f32[1,2048]{1,0:T(1,128)S(1)} %get-tuple-element.15.refs_1_), channel_id=1, source_target_pairs={{0,4},{4,0},{1,5},{5,1},{2,6},{6,2},{3,7},{7,3},{8,12},{12,8},{9,1... | collective-permute-start | bytes 24584 | tf_op jit(solution)/shard_map/ppermute | solution.py:160
  12.1 0.8 %collective-permute-done.refs_2_ = f32[1,2048]{1,0:T(1,128)S(1)} collective-permute-done((f32[1,2048]{1,0:T(1,128)S(1)}, f32[1,2048]{1,0:T(1,128)S(1)}, u32[]{:S(2)}, u32[]{:S(2)}) %collective-permute-start) | collective-permute-done | bytes 8224 | tf_op jit(solution)/shard_map/ppermute | solution.py:160
  12.9 0.8 %scale.2 = (bf16[1024,2048]{1,0:T(8,128)(2,1)S(1)}, f32[1,2048]{1,0:T(1,128)S(1)}) custom-call(f32[1024,2048]{1,0:T(8,128)S(1)} %get-tuple-element.14.refs_0_, f32[1,2048]{1,0:T(1,128)S(1)} %get-tuple-element.15.refs_1_, f32[1,2048]{1,0:T(1,128)S(1)} %collective-permute-done.refs_2_), custom_call_target="tpu_custom_call" | custom-call | flops 419430400 | bytes 2097152 | tf_op jit(solution)/shard_map/scale/pallas_call | solution.py:104
  13.7 0.4 %collective-permute-start.1 = (bf16[1024,2048]{1,0:T(8,128)(2,1)S(1)}, bf16[1024,2048]{1,0:T(8,128)(2,1)S(1)}, u32[]{:S(2)}, u32[]{:S(2)}) collective-permute-start(bf16[1024,2048]{1,0:T(8,128)(2,1)S(1)} %get-tuple-element.16.refs_0_), channel_id=1, source_target_pairs={{0,4},{4,0},{1,5},{5,1},{2,6},{6,2},{3,7},{7,3},{8,12},{12,8},{9,1... | collective-permute-start | bytes 12582920 | tf_op jit(solution)/shard_map/ppermute | solution.py:160
  14.1 10.7 %update.3 = (f32[1024,2048]{1,0:T(8,128)S(1)}, f32[1,2048]{1,0:T(1,128)S(1)}) custom-call(f32[8,128]{1,0:T(8,128)} %bitcast.7, f32[8,128]{1,0:T(8,128)} %bitcast.8, f32[1024,2048]{1,0:T(8,128)} %weight_ref.3, f32[1024,2048]{1,0:T(8,128)} %moment_ref.3, f32[1024,2048]{1,0:T(8,128)} %square_ref.3), custom_call_target="tpu_custom_call" | custom-call | flops 2097152000 | bytes 25165824 | tf_op jit(solution)/shard_map/update/pallas_call | solution.py:64
  24.8 0.2 collective-permute-start.2
  25.0 1.0 %collective-permute-done.2.refs_2_ = f32[1,2048]{1,0:T(1,128)S(1)} collective-permute-done((f32[1,2048]{1,0:T(1,128)S(1)}, f32[1,2048]{1,0:T(1,128)S(1)}, u32[]{:S(2)}, u32[]{:S(2)}) %collective-permute-start.2) | collective-permute-done | bytes 8224 | tf_op jit(solution)/shard_map/ppermute | solution.py:160
  26.0 0.8 %scale.3 = (bf16[1024,2048]{1,0:T(8,128)(2,1)S(1)}, f32[1,2048]{1,0:T(1,128)S(1)}) custom-call(f32[1024,2048]{1,0:T(8,128)S(1)} %get-tuple-element.17.refs_0_, f32[1,2048]{1,0:T(1,128)S(1)} %get-tuple-element.18.refs_1_, f32[1,2048]{1,0:T(1,128)S(1)} %collective-permute-done.2.refs_2_), custom_call_target="tpu_custom_call" | custom-call | flops 419430400 | bytes 2097152 | tf_op jit(solution)/shard_map/scale/pallas_call | solution.py:104
  26.8 0.2 collective-permute-start.3
  27.1 0.6 %copy.14 = f32[2048]{0:T(1024)} copy(f32[2048]{0:T(1024)S(1)} %bitcast.4) | data formatting | bytes 16384
  27.7 0.6 %copy.13 = f32[2048]{0:T(1024)} copy(f32[2048]{0:T(1024)S(1)} %bitcast.3) | data formatting | bytes 16384
  28.3 0.0 collective-permute-done.1.refs_1_
  28.3 4.7 %place.2 = (bf16[2048,2048]{1,0:T(8,128)(2,1)}, bf16[2048,2048]{1,0:T(8,128)(2,1)}) custom-call(bf16[1024,2048]{1,0:T(8,128)(2,1)S(1)} %get-tuple-element.16.refs_0_, bf16[1024,2048]{1,0:T(8,128)(2,1)S(1)} %collective-permute-done.1.refs_1_, bf16[1024,2048]{1,0:T(8,128)(2,1)S(1)} %get-tuple-element.19.refs_2_), custom_call_target="tpu_custom_call" | custom-call | flops 2516582400 | bytes 25165824 | tf_op jit(solution)/shard_map/place/pallas_call | solution.py:135
  33.0 1.1 %collective-permute-done.3.refs_0_ = bf16[1024,2048]{1,0:T(8,128)(2,1)S(1)} collective-permute-done((bf16[1024,2048]{1,0:T(8,128)(2,1)S(1)}, bf16[1024,2048]{1,0:T(8,128)(2,1)S(1)}, u32[]{:S(2)}, u32[]{:S(2)}) %collective-permute-start.3) | collective-permute-done | bytes 4194336 | tf_op jit(solution)/shard_map/ppermute | solution.py:160
  34.1 2.0 %place.3 = bf16[2048,2048]{1,0:T(8,128)(2,1)} custom-call(bf16[1024,2048]{1,0:T(8,128)(2,1)S(1)} %collective-permute-done.3.refs_0_, bf16[2048,2048]{1,0:T(8,128)(2,1)} %get-tuple-element.21.refs_1_), custom_call_target="tpu_custom_call", output_to_operand_aliasing={{}: (1, {})} | custom-call | flops 838860800 | bytes 8388608 | tf_op jit(solution)/shard_map/place/pallas_call | solution.py:135
Async XLA Ops:
  11.3 1.6 %collective-permute-start = (f32[1,2048]{1,0:T(1,128)S(1)}, f32[1,2048]{1,0:T(1,128)S(1)}, u32[]{:S(2)}, u32[]{:S(2)}) collective-permute-start(f32[1,2048]{1,0:T(1,128)S(1)} %get-tuple-element.15.refs_1_), channel_id=1, source_target_pairs={{0,4},{4,0},{1,5},{5,1},{2,6},{6,2},{3,7},{7,3},{8,12},{12,8},{9,1... | collective-permute-start | bytes 24584 | tf_op jit(solution)/shard_map/ppermute | solution.py:160
  13.7 14.6 %collective-permute-start.1 = (bf16[1024,2048]{1,0:T(8,128)(2,1)S(1)}, bf16[1024,2048]{1,0:T(8,128)(2,1)S(1)}, u32[]{:S(2)}, u32[]{:S(2)}) collective-permute-start(bf16[1024,2048]{1,0:T(8,128)(2,1)S(1)} %get-tuple-element.16.refs_0_), channel_id=1, source_target_pairs={{0,4},{4,0},{1,5},{5,1},{2,6},{6,2},{3,7},{7,3},{8,12},{12,8},{9,1... | collective-permute-start | bytes 12582920 | tf_op jit(solution)/shard_map/ppermute | solution.py:160
  24.8 1.2 %collective-permute-start.2 = (f32[1,2048]{1,0:T(1,128)S(1)}, f32[1,2048]{1,0:T(1,128)S(1)}, u32[]{:S(2)}, u32[]{:S(2)}) collective-permute-start(f32[1,2048]{1,0:T(1,128)S(1)} %get-tuple-element.18.refs_1_), channel_id=1, source_target_pairs={{0,4},{4,0},{1,5},{5,1},{2,6},{6,2},{3,7},{7,3},{8,12},{12,8},{9,1... | collective-permute-start | bytes 24584 | tf_op jit(solution)/shard_map/ppermute | solution.py:160
  26.8 7.2 %collective-permute-start.3 = (bf16[1024,2048]{1,0:T(8,128)(2,1)S(1)}, bf16[1024,2048]{1,0:T(8,128)(2,1)S(1)}, u32[]{:S(2)}, u32[]{:S(2)}) collective-permute-start(bf16[1024,2048]{1,0:T(8,128)(2,1)S(1)} %get-tuple-element.19.refs_2_), channel_id=1, source_target_pairs={{0,4},{4,0},{1,5},{5,1},{2,6},{6,2},{3,7},{7,3},{8,12},{12,8},{9,1... | collective-permute-start | bytes 12582920 | tf_op jit(solution)/shard_map/ppermute | solution.py:160

commit v2 on v1

--- a/solution.py
+++ b/solution.py
@@ -13,65 +13,106 @@
 keep_rate = 1.0 - learn_rate * decay_rate
 
 UNITS = 2
-FOLD = 2
+BLOCK = 64
+AHEAD = 8
 LANES = 128
 
 
 def update_kernel(
-    after_ref, gain_ref, weight_ref, moment_ref, square_ref, gained_ref, sums_ref, part_ref, spread_ref, *, block, fold
+    after_ref, gain_ref, weight_ref, moment_ref, square_ref, gained_ref, sums_ref,
+    gains, moments, squares, part_ref, keep_ref, move_ref, sems, gain_sem, *, block, chunk, held
 ):
-    step = pl.program_id(0)
-    width = weight_ref.shape[1]
-
-    def spread(at, slot):
-        for n in range(fold):
-            line = gain_ref[pl.ds(at * fold + n, 1), :]
-            spread_ref[slot, n * block : (n + 1) * block, :] = jnp.broadcast_to(line, (LANES, block)).T
-
-    @pl.when(step == 0)
-    def _():
-        part_ref[...] = jnp.zeros_like(part_ref)
-        spread(0, 0)
-
-    spread(jnp.minimum(step + 1, pl.num_programs(0) - 1), (step + 1) % 2)
-    for n in range(fold):
-        inner = slice(n * block, (n + 1) * block)
-        rows = pl.ds(pl.multiple_of((step * fold + n) * block, block), block)
-        gain = spread_ref[step % 2, inner, :]
-        keep = keep_rate * gain
-        move = learn_rate * gain
-        for at in range(0, width, LANES):
-            lanes = slice(at, at + LANES)
-            square = square_ref[inner, lanes]
-            divisor = square * lax.rsqrt(square) + tiny_value
-            direction = moment_ref[inner, lanes] * lax.rsqrt(divisor * divisor)
-            gained = keep * weight_ref[inner, lanes] - move * direction
-            gained_ref[rows, lanes] = gained
-            part_ref[:, lanes] += jnp.sum(jnp.abs(gained).reshape(block // 8, 8, LANES), axis=0)
-
-    @pl.when(step == pl.num_programs(0) - 1)
-    def _():
-        sums_ref[...] = jnp.sum(part_ref[...], axis=0, keepdims=True)
-
-
-def update(after, gain, weight, moment, square, chunk, width):
+    rows, width = gained_ref.shape
+    count = rows // block
+    columns = pl.ds(chunk * width, width)
+
+    weights = weight_ref if held else gained_ref
+    def copies(at):
+        here = pl.ds(pl.multiple_of(at * block, block), block)
+        return [
+            pltpu.make_async_copy(source.at[here, columns], target.at[here, :], sems.at[n, at])
+            for n, (source, target) in enumerate(
+                ((square_ref, squares), (moment_ref, moments), (weight_ref, gained_ref))[: 2 if held else 3]
+            )
+        ]
+
+    def start(at):
+        for copy in copies(at):
+            copy.start()
+
+    fetch = pltpu.make_async_copy(gain_ref, gains, gain_sem)
+    fetch.start()
+    ahead = min(AHEAD, count)
+    for at in range(ahead):
+        start(at)
+
+    fetch.wait()
+    run = gains.shape[1]
+    for n in range(gains.shape[0]):
+        gain = jnp.broadcast_to(gains[n : n + 1, :], (LANES, run)).T
+        keep_ref[n * run : (n + 1) * run, :] = keep_rate * gain
+        move_ref[n * run : (n + 1) * run, :] = learn_rate * gain
+    part_ref[...] = jnp.zeros_like(part_ref)
+
+    def body(at, _):
+        @pl.when(at + ahead < count)
+        def _():
+            start(at + ahead)
+
+        for copy in copies(at):
+            copy.wait()
+        lanes = [slice(n, n + LANES) for n in range(0, width, LANES)]
+        part = [part_ref[:, tile] for tile in lanes]
+        for row in range(0, block, 8):
+            here = pl.ds(pl.multiple_of(at * block + row, 8), 8)
+            keep = keep_ref[here, :]
+            move = move_ref[here, :]
+            for n, tile in enumerate(lanes):
+                square = squares[here, tile]
+                divisor = square * lax.rsqrt(square) + tiny_value
+                direction = moments[here, tile] * lax.rsqrt(divisor * divisor)
+                gained = keep * weights[here, tile] - move * direction
+                gained_ref[here, tile] = gained
+                part[n] = part[n] + jnp.abs(gained)
+        for n, tile in enumerate(lanes):
+            part_ref[:, tile] = part[n]
+        return 0
+
+    lax.fori_loop(0, count, body, 0)
+    sums_ref[...] = jnp.sum(part_ref[...], axis=0, keepdims=True)
+
+
+def update(after, gain, weight, moment, square, chunk, width, held):
     rows = weight.shape[0]
-    block = min(rows, LANES)
-    fold = FOLD if rows % (block * FOLD) == 0 else 1
-    spec = pl.BlockSpec((block * fold, width), lambda i: (i, chunk))
+    block = BLOCK if rows % BLOCK == 0 else rows
     whole = pl.BlockSpec(memory_space=pltpu.VMEM)
+    far = pl.BlockSpec(memory_space=pl.ANY)
     elements = rows * width
     return pl.pallas_call(
-        functools.partial(update_kernel, block=block, fold=fold),
-        grid=(rows // block // fold,),
-        in_specs=[pl.BlockSpec(memory_space=pl.ANY), whole, spec, spec, spec],
+        functools.partial(update_kernel, block=block, chunk=chunk, held=held),
+        in_specs=[far, far, whole if held else far, far, far],
         out_specs=[whole, whole],
         out_shape=[pltpu.VMEM((rows, width), jnp.float32), pltpu.VMEM((1, width), jnp.float32)],
-        scratch_shapes=[pltpu.VMEM((8, width), jnp.float32), pltpu.VMEM((2, fold * block, LANES), jnp.float32)],
-        compiler_params=pltpu.CompilerParams(vmem_limit_bytes=24 << 20),
+        scratch_shapes=[
+            pltpu.VMEM(gain.shape, jnp.float32),
+            pltpu.VMEM((rows, width), jnp.float32),
+            pltpu.VMEM((rows, width), jnp.float32),
+            pltpu.VMEM((8, width), jnp.float32),
+            pltpu.VMEM((rows, LANES), jnp.float32),
+            pltpu.VMEM((rows, LANES), jnp.float32),
+            pltpu.SemaphoreType.DMA((3, rows // block)),
+            pltpu.SemaphoreType.DMA,
+        ],
+        compiler_params=pltpu.CompilerParams(vmem_limit_bytes=elements * 8 + (3 << 20)),
         cost_estimate=pl.CostEstimate(flops=elements * 1000, bytes_accessed=elements * 12, transcendentals=elements * 2),
         name="update",
-    )(after, *(pltpu.with_memory_space_constraint(array, pltpu.HBM) for array in (gain, weight, moment, square)))
+    )(
+        after,
+        *(
+            pltpu.with_memory_space_constraint(array, pltpu.VMEM if held and n == 1 else pltpu.HBM)
+            for n, array in enumerate((gain, weight, moment, square))
+        ),
+    )
 
 
 def scale_kernel(*refs, total_rows):
@@ -176,7 +217,7 @@
         which, chunk = unit
         if len(history) >= 2:
             ready = finish(*history[len(history) - 2])
-        gained, sums = update(ready, gain, *sources[which], chunk, width)
+        gained, sums = update(ready, gain, *sources[which], chunk, width, chunks == 1 and which == 1)
         history.append((unit, gained, [sums] + rotations(sums)))
     for entry in history[max(len(history) - 2, 0):]:
         finish(*entry)

time: 36.2 us -> 33.5 us (0.925)
  Pallas kernels: 29.6 us -> 26.9 us
    pallas_call x2, Pallas kernels: 21.4 us -> 18.6 us  [update(): pl.pallas_call(functools.partial(update_kernel, block=block, chunk=chunk,...]
    unnamed x2 -> x6, local copies, waits for them, and re-layouts: 1.2 us -> 1.21 us
  transfers between devices with their start and end apart: 4 -> 4, of which waited for: 3 -> 3; matrix products, arithmetic and copies ran while one was open for 3% -> 4% of each run, Pallas kernels for 45% -> 39%
where the time goes in v2:
time: 33.5 us; the launch traced here: 33.3 us
  Pallas kernels  26.9 us (80%)
  waiting for transfers between devices  2.94 us (9%)
  starting transfers between devices  1.61 us (5%)
  local copies, waits for them, and re-layouts  1.21 us (4%)
  between operations  0.69 us (2%)
    pallas_call x2, Pallas kernels, update(): pl.pallas_call(functools.partial(update_kernel, block=block, chunk=chunk,...  18.6 us
    pallas_call x2, Pallas kernels, place(): pl.pallas_call(functools.partial(place_kernel, row_devices=row_devices, c...  6.7 us
    ppermute x4, waiting for transfers between devices, rotations(): lax.ppermute(value, 'rows', [(j, (j + hop) % row_devices) for j in range(...  2.94 us
    ppermute x4, starting transfers between devices, rotations(): lax.ppermute(value, 'rows', [(j, (j + hop) % row_devices) for j in range(...  1.61 us
    pallas_call x2, Pallas kernels, scale(): pl.pallas_call(functools.partial(scale_kernel, total_rows=total_rows), in...  1.56 us
    unnamed x6, local copies, waits for them, and re-layouts  1.21 us
  transfers between devices with their start and end apart: 4, of which 3 were waited for; matrix products, arithmetic and copies ran while one was open for 4% of the time, Pallas kernels for 39%

profile of v2, /device:TPU:3, one launch (start us, length us, event | category | flops | bytes accessed | tf_op | source)
XLA Modules:
  0.0 33.3 jit_solution(968878798753782014)
XLA Ops:
  0.6 0.0 slice-start
  0.6 0.0 slice-start.1
  0.7 11.1 %update.2 = (f32[1024,2048]{1,0:T(8,128)S(1)}, f32[1,2048]{1,0:T(1,128)S(1)}) custom-call(f32[8,128]{1,0:T(8,128)} %bitcast.7, f32[8,128]{1,0:T(8,128)} %bitcast.8, f32[1024,2048]{1,0:T(8,128)} %weight_ref.2, f32[1024,2048]{1,0:T(8,128)} %moment_ref.2, f32[1024,2048]{1,0:T(8,128)} %square_ref.2), custom_call_target="tpu_custom_call" | custom-call | flops 2097152000 | bytes 25165824 | tf_op jit(solution)/shard_map/update/pallas_call | solution.py:91
  11.8 0.7 %collective-permute-start = (f32[1,2048]{1,0:T(1,128)S(1)}, f32[1,2048]{1,0:T(1,128)S(1)}, u32[]{:S(2)}, u32[]{:S(2)}) collective-permute-start(f32[1,2048]{1,0:T(1,128)S(1)} %get-tuple-element.15.refs_1_), channel_id=1, source_target_pairs={{0,4},{4,0},{1,5},{5,1},{2,6},{6,2},{3,7},{7,3},{8,12},{12,8},{9,1... | collective-permute-start | bytes 24584 | tf_op jit(solution)/shard_map/ppermute | solution.py:201
  12.5 0.8 %collective-permute-done.refs_2_ = f32[1,2048]{1,0:T(1,128)S(1)} collective-permute-done((f32[1,2048]{1,0:T(1,128)S(1)}, f32[1,2048]{1,0:T(1,128)S(1)}, u32[]{:S(2)}, u32[]{:S(2)}) %collective-permute-start) | collective-permute-done | bytes 8224 | tf_op jit(solution)/shard_map/ppermute | solution.py:201
  13.3 0.8 %scale.2 = (bf16[1024,2048]{1,0:T(8,128)(2,1)S(1)}, f32[1,2048]{1,0:T(1,128)S(1)}) custom-call(f32[1024,2048]{1,0:T(8,128)S(1)} %get-tuple-element.14.refs_0_, f32[1,2048]{1,0:T(1,128)S(1)} %get-tuple-element.15.refs_1_, f32[1,2048]{1,0:T(1,128)S(1)} %collective-permute-done.refs_2_), custom_call_target="tpu_custom_call" | custom-call | flops 419430400 | bytes 2097152 | tf_op jit(solution)/shard_map/scale/pallas_call | solution.py:145
  14.1 0.4 %collective-permute-start.1 = (bf16[1024,2048]{1,0:T(8,128)(2,1)S(1)}, bf16[1024,2048]{1,0:T(8,128)(2,1)S(1)}, u32[]{:S(2)}, u32[]{:S(2)}) collective-permute-start(bf16[1024,2048]{1,0:T(8,128)(2,1)S(1)} %get-tuple-element.16.refs_0_), channel_id=1, source_target_pairs={{0,4},{4,0},{1,5},{5,1},{2,6},{6,2},{3,7},{7,3},{8,12},{12,8},{9,1... | collective-permute-start | bytes 12582920 | tf_op jit(solution)/shard_map/ppermute | solution.py:201
  14.5 0.0 slice-done
  14.5 0.0 slice-done.1
  14.5 7.5 %update.3 = (f32[1024,2048]{1,0:T(8,128)S(1)}, f32[1,2048]{1,0:T(1,128)S(1)}) custom-call(f32[8,128]{1,0:T(8,128)} %bitcast.9, f32[8,128]{1,0:T(8,128)} %bitcast.10, f32[1024,2048]{1,0:T(8,128)S(1)} %bitcast.6, f32[1024,2048]{1,0:T(8,128)} %moment_ref.3, f32[1024,2048]{1,0:T(8,128)} %square_ref.3), custom_call_target="tpu_custom_call" | custom-call | flops 2097152000 | bytes 25165824 | tf_op jit(solution)/shard_map/update/pallas_call | solution.py:91
  22.0 0.2 collective-permute-start.2
  22.3 1.0 %collective-permute-done.2.refs_2_ = f32[1,2048]{1,0:T(1,128)S(1)} collective-permute-done((f32[1,2048]{1,0:T(1,128)S(1)}, f32[1,2048]{1,0:T(1,128)S(1)}, u32[]{:S(2)}, u32[]{:S(2)}) %collective-permute-start.2) | collective-permute-done | bytes 8224 | tf_op jit(solution)/shard_map/ppermute | solution.py:201
  23.3 0.8 %scale.3 = (bf16[1024,2048]{1,0:T(8,128)(2,1)S(1)}, f32[1,2048]{1,0:T(1,128)S(1)}) custom-call(f32[1024,2048]{1,0:T(8,128)S(1)} %get-tuple-element.17.refs_0_, f32[1,2048]{1,0:T(1,128)S(1)} %get-tuple-element.18.refs_1_, f32[1,2048]{1,0:T(1,128)S(1)} %collective-permute-done.2.refs_2_), custom_call_target="tpu_custom_call" | custom-call | flops 419430400 | bytes 2097152 | tf_op jit(solution)/shard_map/scale/pallas_call | solution.py:145
  24.1 0.2 collective-permute-start.3
  24.3 0.6 %copy.14 = f32[2048]{0:T(1024)} copy(f32[2048]{0:T(1024)S(1)} %bitcast.4) | data formatting | bytes 16384
  24.9 0.6 %copy.13 = f32[2048]{0:T(1024)} copy(f32[2048]{0:T(1024)S(1)} %bitcast.3) | data formatting | bytes 16384
  25.5 0.0 collective-permute-done.1.refs_1_
  25.5 4.7 %place.2 = (bf16[2048,2048]{1,0:T(8,128)(2,1)}, bf16[2048,2048]{1,0:T(8,128)(2,1)}) custom-call(bf16[1024,2048]{1,0:T(8,128)(2,1)S(1)} %get-tuple-element.16.refs_0_, bf16[1024,2048]{1,0:T(8,128)(2,1)S(1)} %collective-permute-done.1.refs_1_, bf16[1024,2048]{1,0:T(8,128)(2,1)S(1)} %get-tuple-element.19.refs_2_), custom_call_target="tpu_custom_call" | custom-call | flops 2516582400 | bytes 25165824 | tf_op jit(solution)/shard_map/place/pallas_call | solution.py:176
  30.2 1.1 %collective-permute-done.3.refs_0_ = bf16[1024,2048]{1,0:T(8,128)(2,1)S(1)} collective-permute-done((bf16[1024,2048]{1,0:T(8,128)(2,1)S(1)}, bf16[1024,2048]{1,0:T(8,128)(2,1)S(1)}, u32[]{:S(2)}, u32[]{:S(2)}) %collective-permute-start.3) | collective-permute-done | bytes 4194336 | tf_op jit(solution)/shard_map/ppermute | solution.py:201
  31.3 2.0 %place.3 = bf16[2048,2048]{1,0:T(8,128)(2,1)} custom-call(bf16[1024,2048]{1,0:T(8,128)(2,1)S(1)} %collective-permute-done.3.refs_0_, bf16[2048,2048]{1,0:T(8,128)(2,1)} %get-tuple-element.21.refs_1_), custom_call_target="tpu_custom_call", output_to_operand_aliasing={{}: (1, {})} | custom-call | flops 838860800 | bytes 8388608 | tf_op jit(solution)/shard_map/place/pallas_call | solution.py:176
  (1 shorter events, 0.0 us)
Async XLA Ops:
  0.6 13.9 %slice-start = ((s8[8388608]{0:T(1024)(128)(4,1)}), s8[4194304]{0:T(1024)(128)(4,1)S(1)}, s32[]{:S(2)}) async-start(s8[8388608]{0:T(1024)(128)(4,1)} %bitcast.5), calls=%async_computation | async-start | bytes 8388608
  0.6 13.9 %slice-start.1 = ((s8[8388608]{0:T(1024)(128)(4,1)}), s8[4194304]{0:T(1024)(128)(4,1)S(1)}, s32[]{:S(2)}) async-start(s8[8388608]{0:T(1024)(128)(4,1)} %bitcast.5), calls=%async_computation.1 | async-start | bytes 8388608
  11.8 1.6 %collective-permute-start = (f32[1,2048]{1,0:T(1,128)S(1)}, f32[1,2048]{1,0:T(1,128)S(1)}, u32[]{:S(2)}, u32[]{:S(2)}) collective-permute-start(f32[1,2048]{1,0:T(1,128)S(1)} %get-tuple-element.15.refs_1_), channel_id=1, source_target_pairs={{0,4},{4,0},{1,5},{5,1},{2,6},{6,2},{3,7},{7,3},{8,12},{12,8},{9,1... | collective-permute-start | bytes 24584 | tf_op jit(solution)/shard_map/ppermute | solution.py:201
  14.1 11.4 %collective-permute-start.1 = (bf16[1024,2048]{1,0:T(8,128)(2,1)S(1)}, bf16[1024,2048]{1,0:T(8,128)(2,1)S(1)}, u32[]{:S(2)}, u32[]{:S(2)}) collective-permute-start(bf16[1024,2048]{1,0:T(8,128)(2,1)S(1)} %get-tuple-element.16.refs_0_), channel_id=1, source_target_pairs={{0,4},{4,0},{1,5},{5,1},{2,6},{6,2},{3,7},{7,3},{8,12},{12,8},{9,1... | collective-permute-start | bytes 12582920 | tf_op jit(solution)/shard_map/ppermute | solution.py:201
  22.0 1.2 %collective-permute-start.2 = (f32[1,2048]{1,0:T(1,128)S(1)}, f32[1,2048]{1,0:T(1,128)S(1)}, u32[]{:S(2)}, u32[]{:S(2)}) collective-permute-start(f32[1,2048]{1,0:T(1,128)S(1)} %get-tuple-element.18.refs_1_), channel_id=1, source_target_pairs={{0,4},{4,0},{1,5},{5,1},{2,6},{6,2},{3,7},{7,3},{8,12},{12,8},{9,1... | collective-permute-start | bytes 24584 | tf_op jit(solution)/shard_map/ppermute | solution.py:201
  24.1 7.2 %collective-permute-start.3 = (bf16[1024,2048]{1,0:T(8,128)(2,1)S(1)}, bf16[1024,2048]{1,0:T(8,128)(2,1)S(1)}, u32[]{:S(2)}, u32[]{:S(2)}) collective-permute-start(bf16[1024,2048]{1,0:T(8,128)(2,1)S(1)} %get-tuple-element.19.refs_2_), channel_id=1, source_target_pairs={{0,4},{4,0},{1,5},{5,1},{2,6},{6,2},{3,7},{7,3},{8,12},{12,8},{9,1... | collective-permute-start | bytes 12582920 | tf_op jit(solution)/shard_map/ppermute | solution.py:201
